TPU v7x, 32 devices: a whole 2x2x4 slice. The times are simulated.
32 devices in a mesh: section: 2 (over core), expert: 16 (over z, y, x).
Axes of the slice: x: 2, y: 2, z: 4, core: 2. Of those that a mesh axis runs over, the one named last changes fastest.
Arguments:
- tokens: bfloat16 [2, 1024, 2048], P(None, 'expert'), may hold values from -6 to 6
- norm_gain: float32 [2, 2048], P('section'), may hold values from 0.5 to 2
- gate_weight: bfloat16 [2, 16, 2048, 768], P('section', 'expert'), may hold values from -0.125 to 0.125
- up_weight: bfloat16 [2, 16, 2048, 768], P('section', 'expert'), may hold values from -0.125 to 0.125
- down_weight: bfloat16 [2, 16, 768, 2048], P('section', 'expert'), may hold values from -0.21875 to 0.21875
- expert_place: int32 [2, 16], P('section'), may hold values from 0 to 15, each once within a row
- expert_ids: int32 [2, 2, 1024, 8], P('section', None, 'expert'), may hold values from 0 to 15, all different within a row; in each aligned block of 64 rows (0 to 63, 64 to 127, ..., all dimensions but the last counted through in order) at most 40 rows name the same one
- route_weights: float32 [2, 2, 1024, 8], P('section', None, 'expert'), may hold values from 0.05 to 0.4
Outputs:
- final_states: bfloat16 [2, 1024, 2048], P(None, 'expert')
Inputs may be any that keep to these rules, and one draw needn't show every extreme that they name: `expert_ids`: each row names 8 different experts. In each aligned block of 64 rows (one device's tokens of one micro-batch in one layer) no expert is named by more than 40 rows, a bound that some block reaches. `expert_place`: each layer's row names every index along expert once.
All inputs are finite; a program needn't handle non-finite values.
Results may differ from a plain program's by a relative error of at most 0.013.
Values may be sent and summed in bfloat16 or wider, within the bound.
A program may use at most 128 MiB of HBM per device.

v0:
```python
import functools

import jax
import jax.numpy as jnp
from jax import lax
from jax.experimental import pallas as pl
from jax.experimental.pallas import tpu as pltpu
from jax.sharding import PartitionSpec as P

EPSILON = 1e-06


def from_behind(array, axis, by):
    size = lax.axis_size(axis)
    return lax.ppermute(array, axis, [(i, (i + by) % size) for i in range(size)])


def normalize(values, gain_row):
    widened = values.astype(jnp.float32)
    inverse_rms = lax.rsqrt(jnp.mean(widened * widened, axis=-1, keepdims=True) + EPSILON)
    return (widened * inverse_rms * gain_row[None, :]).astype(jnp.bfloat16)


def expert_ffn(row_block, gate_matrix, up_matrix, down_matrix):
    gate_part = jnp.dot(row_block, gate_matrix, preferred_element_type=jnp.float32)
    up_part = jnp.dot(row_block, up_matrix, preferred_element_type=jnp.float32)
    hidden_units = (jax.nn.silu(gate_part) * up_part).astype(jnp.bfloat16)
    return jnp.dot(hidden_units, down_matrix, preferred_element_type=jnp.float32).astype(
        jnp.bfloat16
    )


def routed_local(
    tokens, norm_gain, gate_weight, up_weight, down_weight, expert_place, expert_ids, route_weights
):
    sections = lax.axis_size("section")
    groups = lax.axis_size("expert")
    section_index = lax.axis_index("section")
    micro_count = tokens.shape[0]
    tok_rows = tokens.shape[1]
    model_width = tokens.shape[2]
    top_count = expert_ids.shape[3]
    experts_all = expert_place.shape[1]
    capacity = max(2, 5 * tok_rows * top_count // (4 * experts_all))
    expert_lanes = jnp.arange(experts_all, dtype=jnp.int32)
    flat_token = jnp.arange(tok_rows * top_count, dtype=jnp.int32) // top_count
    own_params = (
        norm_gain[0],
        gate_weight[0, 0],
        up_weight[0, 0],
        down_weight[0, 0],
        expert_place[0],
        expert_ids[0],
        route_weights[0],
    )

    def run_rows(received, active, params):
        row_shape = received.shape
        flat_rows = received.reshape(-1, model_width)
        computed = lax.cond(
            active,
            lambda row_block: expert_ffn(row_block, params[1], params[2], params[3]),
            lambda row_block: jnp.zeros_like(row_block),
            flat_rows,
        )
        return computed.reshape(row_shape)

    def layer_step(hidden, micro_index, active, params):
        normed = normalize(hidden, params[0])
        holder_table = params[4]
        chosen = lax.dynamic_index_in_dim(params[5], micro_index, 0, keepdims=False).reshape(-1)
        weights = lax.dynamic_index_in_dim(params[6], micro_index, 0, keepdims=False)
        onehot = (chosen[:, None] == expert_lanes[None, :]).astype(jnp.int32)
        before = jnp.cumsum(onehot, axis=0) - onehot
        position = jnp.sum(before * onehot, axis=1)
        holder = jnp.sum(onehot * holder_table[None, :], axis=1)
        target = holder * capacity + position
        outgoing = (
            jnp.zeros((groups * capacity, model_width), jnp.bfloat16)
            .at[target]
            .set(normed[flat_token])
        )
        outgoing = outgoing.reshape(groups, capacity, model_width)
        received = lax.all_to_all(outgoing, "expert", split_axis=0, concat_axis=0, tiled=True)
        returned_rows = lax.all_to_all(
            run_rows(received, active, params), "expert", split_axis=0, concat_axis=0, tiled=True
        )
        picked = returned_rows.reshape(groups * capacity, model_width)[target]
        picked = picked.astype(jnp.float32).reshape(tok_rows, top_count, model_width)
        mixture = jnp.einsum("tk,tkd->td", weights, picked)
        return (hidden.astype(jnp.float32) + mixture).astype(jnp.bfloat16)

    other_mats = from_behind((own_params[1], own_params[2], own_params[3]), "section", 1)
    other_ints = from_behind((own_params[4], own_params[5]), "section", 1)
    other_floats = from_behind((own_params[0], own_params[6]), "section", 1)
    other_params = (
        other_floats[0],
        other_mats[0],
        other_mats[1],
        other_mats[2],
        other_ints[0],
        other_ints[1],
        other_floats[1],
    )
    is_first = section_index == 0
    first_params = tuple(
        (jnp.where(is_first, mine, theirs) for mine, theirs in zip(own_params, other_params))
    )
    second_params = tuple(
        (jnp.where(is_first, theirs, mine) for mine, theirs in zip(own_params, other_params))
    )
    share = micro_count // sections
    always = jnp.array(True)
    micro_index = section_index * share + 0
    hidden = lax.dynamic_index_in_dim(tokens, micro_index, 0, keepdims=False)
    hidden = layer_step(hidden, micro_index, always, first_params)
    hidden = layer_step(hidden, micro_index, always, second_params)
    own_finals = [hidden]
    return lax.all_gather(jnp.stack(own_finals), "section", axis=0, tiled=True)


def layer_kernel(
    layer,
    depth,
    normed_ref,
    hidden_ref,
    gate_hbm,
    up_hbm,
    down_hbm,
    out_ref,
    gate_mat,
    up_mat,
    down_mat,
    held,
    parts,
    from_x_half,
    from_y_half,
    from_x,
    from_y,
    from_z,
    sends,
    arrivals,
    mat_sends,
    mat_arrivals,
):
    section = lax.axis_index("section")
    me = lax.axis_index("expert")
    level = me // 4
    plane = lax.rem(me, 4)
    beside_x = level * 4 + plane + 1 - 2 * lax.rem(plane, 2)
    beside_y = level * 4 + lax.rem(plane + 2, 4)
    rows = normed_ref.shape[0]
    half = rows // 2

    def at_level(offset):
        return lax.rem(level + offset + depth, depth) * 4 + plane

    barrier = pltpu.get_barrier_semaphore()
    partners = [{"expert": beside_x}, {"expert": beside_y}, {"section": 1 - section}]
    partners += [{"expert": at_level(k)} for k in range(1, depth)]
    for partner in partners:
        pl.semaphore_signal(
            barrier, inc=1, device_id=partner, device_id_type=pl.DeviceIdType.MESH
        )
    pl.semaphore_wait(barrier, len(partners))

    started = []

    def send(kind, k, source, target, peer):
        copy = pltpu.make_async_remote_copy(
            src_ref=source,
            dst_ref=target,
            send_sem=sends.at[kind, k],
            recv_sem=arrivals.at[kind, k],
            device_id={"expert": peer},
            device_id_type=pl.DeviceIdType.MESH,
        )
        copy.start()
        started.append(copy)
        return copy

    lower, upper = pl.ds(0, half), pl.ds(half, rows - half)

    by_z = [None] + [
        send(0, k, normed_ref, held.at[k, 0], at_level(k)) for k in range(1, depth)
    ]
    by_x = {0: send(1, 0, normed_ref, held.at[0, 1], beside_x)}
    by_y = {0: send(2, 0, normed_ref, held.at[0, 2], beside_y)}

    mats = [(gate_hbm, gate_mat), (up_hbm, up_mat), (down_hbm, down_mat)]
    remote_mats = [
        pltpu.make_async_remote_copy(
            src_ref=source,
            dst_ref=target,
            send_sem=mat_sends.at[i],
            recv_sem=mat_arrivals.at[i],
            device_id={"section": 1 - section},
            device_id_type=pl.DeviceIdType.MESH,
        )
        for i, (source, target) in enumerate(mats)
    ]
    local_mats = [
        pltpu.make_async_copy(source, target, mat_sends.at[3 + i])
        for i, (source, target) in enumerate(mats)
    ]

    @pl.when(section == layer)
    def _():
        for copy in remote_mats + local_mats:
            copy.start()

    held[0, 0] = normed_ref[...]

    by_xy, by_yx = {}, {}

    def relay(k):
        by_z[k].wait_recv()
        by_x[k] = send(1, k, held.at[k, 0], held.at[k, 1], beside_x)
        by_y[k] = send(2, k, held.at[k, 0], held.at[k, 2], beside_y)

    def relay_diagonal(k):
        by_x[k].wait_recv()
        by_xy[k] = send(3, k, held.at[k, 1, lower], held.at[k, 3, lower], beside_y)
        by_y[k].wait_recv()
        by_yx[k] = send(4, k, held.at[k, 2, upper], held.at[k, 3, upper], beside_x)

    halves_y, halves_x, fulls_x, fulls_y, backs = {}, {}, {}, {}, {}

    def compute(k):
        by_xy[k].wait_recv()
        by_yx[k].wait_recv()
        width = hidden_ref.shape[1]
        block = held[k, :, :, 0:width].reshape(4 * rows, width)
        tags = held[k, :, :, width:].reshape(4 * rows, held.shape[3] - width)
        lane = lax.broadcasted_iota(jnp.int32, tags.shape, 1)
        named = (lane == me) | (lane == me + 4 * depth)
        share = jnp.sum(jnp.where(named, tags.astype(jnp.float32), 0.0), axis=1, keepdims=True)
        gate_part = jnp.dot(block, gate_mat[...], preferred_element_type=jnp.float32)
        up_part = jnp.dot(block, up_mat[...], preferred_element_type=jnp.float32)
        hidden_units = (gate_part / (1.0 + jnp.exp(-gate_part)) * up_part).astype(jnp.bfloat16)
        out = jnp.dot(hidden_units, down_mat[...], preferred_element_type=jnp.float32)
        out = out.astype(jnp.bfloat16).astype(jnp.float32) * share
        parts[k] = out.astype(jnp.bfloat16).reshape(parts.shape[1:])
        halves_y[k] = send(5, k, parts.at[k, 3, lower], from_y_half.at[k], beside_y)
        halves_x[k] = send(6, k, parts.at[k, 3, upper], from_x_half.at[k], beside_x)

    def add(*terms):
        total = terms[0].astype(jnp.float32)
        for term in terms[1:]:
            total = total + term.astype(jnp.float32)
        return total

    def combine_half(k):
        halves_y[k].wait_recv()
        parts[k, 1, lower] = add(parts[k, 1, lower], from_y_half[k]).astype(jnp.bfloat16)
        fulls_x[k] = send(7, k, parts.at[k, 1], from_x.at[k], beside_x)
        halves_x[k].wait_recv()
        parts[k, 2, upper] = add(parts[k, 2, upper], from_x_half[k]).astype(jnp.bfloat16)
        fulls_y[k] = send(8, k, parts.at[k, 2], from_y.at[k], beside_y)

    def combine_full(k):
        fulls_x[k].wait_recv()
        fulls_y[k].wait_recv()
        parts[k, 0] = add(parts[k, 0], from_x[k], from_y[k]).astype(jnp.bfloat16)
        backs[k] = send(9, k, parts.at[k, 0], from_z.at[k], at_level(-k))

    def wait_mats():
        @pl.when(section == layer)
        def _():
            for copy in remote_mats:
                copy.wait_send()
            for copy in local_mats:
                copy.wait()

        @pl.when(section != layer)
        def _():
            for copy in remote_mats:
                copy.wait_recv()

    relay(1)
    relay_diagonal(0)
    for k in range(depth):
        if k + 2 < depth:
            relay(k + 2)
        if k + 1 < depth:
            relay_diagonal(k + 1)
        if k == 0:
            wait_mats()
        compute(k)
        if k >= 1:
            combine_half(k - 1)
        if k >= 2:
            if k > 2:
                combine_full(k - 2)
    combine_half(depth - 1)
    for k in range(max(1, depth - 2), depth):
        combine_full(k)
    fulls_x[0].wait_recv()
    fulls_y[0].wait_recv()
    mixture = add(parts[0, 0], from_x[0], from_y[0])
    for k in range(1, depth):
        backs[k].wait_recv()
        mixture = mixture + from_z[k].astype(jnp.float32)
    out_ref[...] = (hidden_ref[...].astype(jnp.float32) + mixture).astype(jnp.bfloat16)
    for copy in started:
        copy.wait_send()


def layer_call(layer, depth, normed, hidden, gate_matrix, up_matrix, down_matrix):
    rows, width = hidden.shape
    vmem = pl.BlockSpec(memory_space=pltpu.VMEM)
    anywhere = pl.BlockSpec(memory_space=pl.ANY)
    bf16 = jnp.bfloat16
    return pl.pallas_call(
        functools.partial(layer_kernel, layer, depth),
        out_shape=jax.ShapeDtypeStruct((rows, width), bf16),
        in_specs=[vmem, vmem, anywhere, anywhere, anywhere],
        out_specs=vmem,
        scratch_shapes=[
            pltpu.VMEM(gate_matrix.shape, bf16),
            pltpu.VMEM(up_matrix.shape, bf16),
            pltpu.VMEM(down_matrix.shape, bf16),
            pltpu.VMEM((depth, 4, rows, normed.shape[1]), bf16),
            pltpu.VMEM((depth, 4, rows, width), bf16),
            pltpu.VMEM((depth, rows // 2, width), bf16),
            pltpu.VMEM((depth, rows // 2, width), bf16),
            pltpu.VMEM((depth, rows, width), bf16),
            pltpu.VMEM((depth, rows, width), bf16),
            pltpu.VMEM((depth, rows, width), bf16),
            pltpu.SemaphoreType.DMA((10, depth)),
            pltpu.SemaphoreType.DMA((10, depth)),
            pltpu.SemaphoreType.DMA((6,)),
            pltpu.SemaphoreType.DMA((3,)),
        ],
        compiler_params=pltpu.CompilerParams(
            collective_id=layer,
            has_side_effects=True,
            vmem_limit_bytes=56 * 1024 * 1024,
        ),
    )(normed, hidden, gate_matrix, up_matrix, down_matrix)


def dense_local(
    tokens, norm_gain, gate_weight, up_weight, down_weight, expert_place, expert_ids, route_weights
):
    groups = lax.axis_size("expert")
    section_index = lax.axis_index("section")
    is_first = section_index == 0
    lanes = jnp.arange(groups, dtype=jnp.int32)
    held_by = jnp.sum(
        jnp.where(expert_ids[0][..., None] == lanes, expert_place[0], 0), axis=-1
    )
    dense = jnp.sum(
        jnp.where(held_by[..., None] == lanes, route_weights[0][..., None], 0.0), axis=2
    )
    kept = jnp.where(is_first, dense[0], dense[1])
    sent = jnp.where(is_first, dense[1], dense[0])
    swapped = from_behind(sent, "section", 1)
    both = jnp.stack([jnp.where(is_first, kept, swapped), jnp.where(is_first, swapped, kept)])
    high = lax.reduce_precision(both, 8, 7)
    room = -(2 * groups) % 128
    tags = jnp.concatenate(
        [high, both - high, jnp.zeros(both.shape[:2] + (room,), jnp.float32)], axis=2
    ).astype(jnp.bfloat16)

    other_gain = from_behind(norm_gain[0], "section", 1)
    gains = (
        jnp.where(is_first, norm_gain[0], other_gain),
        jnp.where(is_first, other_gain, norm_gain[0]),
    )
    depth = groups // 4
    hidden = lax.dynamic_index_in_dim(tokens, section_index, 0, keepdims=False)
    for layer in range(2):
        normed = normalize(hidden, gains[layer])
        hidden = layer_call(
            layer,
            depth,
            jnp.concatenate([normed, tags[layer]], axis=1),
            hidden,
            gate_weight[0, 0],
            up_weight[0, 0],
            down_weight[0, 0],
        )
    return lax.all_gather(hidden[None], "section", axis=0, tiled=True)


def local(
    tokens, norm_gain, gate_weight, up_weight, down_weight, expert_place, expert_ids, route_weights
):
    dense = 2 * expert_ids.shape[3] >= expert_place.shape[1] and tokens.shape[0] == 2
    dense = dense and lax.axis_size("expert") % 4 == 0 and lax.axis_size("expert") > 4
    run = dense_local if dense else routed_local
    return run(
        tokens,
        norm_gain,
        gate_weight,
        up_weight,
        down_weight,
        expert_place,
        expert_ids,
        route_weights,
    )


def solution(mesh):
    in_specs = (
        P(None, "expert", None),
        P("section", None),
        P("section", "expert", None, None),
        P("section", "expert", None, None),
        P("section", "expert", None, None),
        P("section", None),
        P("section", None, "expert", None),
        P("section", None, "expert", None),
    )
    out_specs = P(None, "expert", None)
    return jax.shard_map(local, mesh=mesh, in_specs=in_specs, out_specs=out_specs, check_vma=False)
```

profile of v0, /device:TPU:0, one launch (start us, length us, event | category | flops | bytes accessed | tf_op | source)
XLA Modules:
  0.0 200.9 jit_solution(12168199420507045988)
XLA Ops:
  0.0 0.8 select_reduce_fusion.1
  0.8 0.7 select_reduce_fusion
  1.6 0.6 collective-permute-start.1
  2.1 0.1 collective-permute-start
  2.2 1.1 fusion
  3.3 0.0 copy-start
  3.3 0.1 pad.6.clone
  3.4 0.0 collective-permute-done.1
  3.4 0.1 copy.17
  3.5 0.1 copy.18
  3.6 0.1 maximum_maximum_fusion
  3.7 0.0 collective-permute-done
  3.7 0.7 broadcast_select_fusion
  4.4 0.1 fusion.2
  4.6 0.7 pad_maximum_fusion.normed_ref
  5.3 0.0 copy-done
  5.3 97.2 %shard_map.82.hidden_ref = bf16[64,2048]{1,0:T(8,128)(2,1)} custom-call(bf16[64,2176]{1,0:T(8,128)(2,1)} %pad_maximum_fusion.normed_ref, bf16[64,2048]{1,0:T(8,128)(2,1)} %copy-done, bf16[2048,768]{1,0:T(8,128)(2,1)} %bitcast.28, bf16[2048,768]{1,0:T(8,128)(2,1)} %bitcast.30, bf16[768,2048]{1,0:T(8,128)(2,1)} %bitcast.32), custom_call_target="tpu_custom_call" | custom-call | tf_op jit(solution)/shard_map/pallas_call | solution.py:314
  102.5 1.1 fusion.3
  103.6 1.1 fusion.5
  104.7 0.7 pad_maximum_fusion.1.normed_ref
  105.5 92.3 %shard_map.83 = bf16[64,2048]{1,0:T(8,128)(2,1)} custom-call(bf16[64,2176]{1,0:T(8,128)(2,1)} %pad_maximum_fusion.1.normed_ref, bf16[64,2048]{1,0:T(8,128)(2,1)} %shard_map.82.hidden_ref, bf16[2048,768]{1,0:T(8,128)(2,1)} %bitcast.29, bf16[2048,768]{1,0:T(8,128)(2,1)} %bitcast.31, bf16[768,2048]{1,0:T(8,128)(2,1)} %bitcast.33), custom_call_target="tpu_custom_call" | custom-call | tf_op jit(solution)/shard_map/pallas_call | solution.py:314
  197.8 2.4 %all-gather = bf16[128,2048]{1,0:T(8,128)(2,1)S(1)} all-gather(bf16[64,2048]{1,0:T(8,128)(2,1)} %shard_map.83), channel_id=2, replica_groups=mesh['section'=2,'expert'=16] {'section'}, dimensions={0}, use_global_device_ids=true | all-gather | bytes 786432 | tf_op jit(solution)/shard_map/all_gather | solution.py:384
  200.1 0.8 copy.21
  (8 shorter events, 0.1 us)
Async XLA Ops:
  1.6 1.9 collective-permute-start.1
  2.1 1.6 collective-permute-start
  3.3 2.0 copy-start
where the time goes:
time: 201 us
  Pallas kernels  189 us (94%)
  other arithmetic  7.25 us (4%)
  blocking collectives  2.39 us (1%)
    pallas_call x2, Pallas kernels, layer_call(): pl.pallas_call(functools.partial(layer_kernel, layer, depth), out_shape=j...  189 us
  transfers between devices with their start and end apart: 2, of which 0 were waited for; matrix products, arithmetic and copies ran while one was open for 1% of the time, Pallas kernels for 0%

commit v1 on v0

v1 whole, which is shorter than its diff:
```python
import functools

import jax
import jax.numpy as jnp
from jax import lax
from jax.experimental import pallas as pl
from jax.experimental.pallas import tpu as pltpu
from jax.sharding import PartitionSpec as P

EPSILON = 1e-06


def from_behind(array, axis, by):
    size = lax.axis_size(axis)
    return lax.ppermute(array, axis, [(i, (i + by) % size) for i in range(size)])


def normalize(values, gain_row):
    widened = values.astype(jnp.float32)
    inverse_rms = lax.rsqrt(jnp.mean(widened * widened, axis=-1, keepdims=True) + EPSILON)
    return (widened * inverse_rms * gain_row[None, :]).astype(jnp.bfloat16)


def expert_ffn(row_block, gate_matrix, up_matrix, down_matrix):
    gate_part = jnp.dot(row_block, gate_matrix, preferred_element_type=jnp.float32)
    up_part = jnp.dot(row_block, up_matrix, preferred_element_type=jnp.float32)
    hidden_units = (jax.nn.silu(gate_part) * up_part).astype(jnp.bfloat16)
    return jnp.dot(hidden_units, down_matrix, preferred_element_type=jnp.float32).astype(
        jnp.bfloat16
    )


def routed_local(
    tokens, norm_gain, gate_weight, up_weight, down_weight, expert_place, expert_ids, route_weights
):
    sections = lax.axis_size("section")
    groups = lax.axis_size("expert")
    section_index = lax.axis_index("section")
    micro_count = tokens.shape[0]
    tok_rows = tokens.shape[1]
    model_width = tokens.shape[2]
    top_count = expert_ids.shape[3]
    experts_all = expert_place.shape[1]
    capacity = max(2, 5 * tok_rows * top_count // (4 * experts_all))
    expert_lanes = jnp.arange(experts_all, dtype=jnp.int32)
    flat_token = jnp.arange(tok_rows * top_count, dtype=jnp.int32) // top_count
    own_params = (
        norm_gain[0],
        gate_weight[0, 0],
        up_weight[0, 0],
        down_weight[0, 0],
        expert_place[0],
        expert_ids[0],
        route_weights[0],
    )

    def run_rows(received, active, params):
        row_shape = received.shape
        flat_rows = received.reshape(-1, model_width)
        computed = lax.cond(
            active,
            lambda row_block: expert_ffn(row_block, params[1], params[2], params[3]),
            lambda row_block: jnp.zeros_like(row_block),
            flat_rows,
        )
        return computed.reshape(row_shape)

    def layer_step(hidden, micro_index, active, params):
        normed = normalize(hidden, params[0])
        holder_table = params[4]
        chosen = lax.dynamic_index_in_dim(params[5], micro_index, 0, keepdims=False).reshape(-1)
        weights = lax.dynamic_index_in_dim(params[6], micro_index, 0, keepdims=False)
        onehot = (chosen[:, None] == expert_lanes[None, :]).astype(jnp.int32)
        before = jnp.cumsum(onehot, axis=0) - onehot
        position = jnp.sum(before * onehot, axis=1)
        holder = jnp.sum(onehot * holder_table[None, :], axis=1)
        target = holder * capacity + position
        outgoing = (
            jnp.zeros((groups * capacity, model_width), jnp.bfloat16)
            .at[target]
            .set(normed[flat_token])
        )
        outgoing = outgoing.reshape(groups, capacity, model_width)
        received = lax.all_to_all(outgoing, "expert", split_axis=0, concat_axis=0, tiled=True)
        returned_rows = lax.all_to_all(
            run_rows(received, active, params), "expert", split_axis=0, concat_axis=0, tiled=True
        )
        picked = returned_rows.reshape(groups * capacity, model_width)[target]
        picked = picked.astype(jnp.float32).reshape(tok_rows, top_count, model_width)
        mixture = jnp.einsum("tk,tkd->td", weights, picked)
        return (hidden.astype(jnp.float32) + mixture).astype(jnp.bfloat16)

    other_mats = from_behind((own_params[1], own_params[2], own_params[3]), "section", 1)
    other_ints = from_behind((own_params[4], own_params[5]), "section", 1)
    other_floats = from_behind((own_params[0], own_params[6]), "section", 1)
    other_params = (
        other_floats[0],
        other_mats[0],
        other_mats[1],
        other_mats[2],
        other_ints[0],
        other_ints[1],
        other_floats[1],
    )
    is_first = section_index == 0
    first_params = tuple(
        (jnp.where(is_first, mine, theirs) for mine, theirs in zip(own_params, other_params))
    )
    second_params = tuple(
        (jnp.where(is_first, theirs, mine) for mine, theirs in zip(own_params, other_params))
    )
    share = micro_count // sections
    always = jnp.array(True)
    micro_index = section_index * share + 0
    hidden = lax.dynamic_index_in_dim(tokens, micro_index, 0, keepdims=False)
    hidden = layer_step(hidden, micro_index, always, first_params)
    hidden = layer_step(hidden, micro_index, always, second_params)
    own_finals = [hidden]
    return lax.all_gather(jnp.stack(own_finals), "section", axis=0, tiled=True)


def cascade_kernel(
    depth,
    cap,
    tokens_ref,
    gain_ref,
    dense_ref,
    gate_hbm,
    up_hbm,
    down_hbm,
    out_ref,
    gate_mats,
    up_mats,
    down_mats,
    other_gain,
    other_dense,
    meta,
    blocks,
    picks,
    held,
    outs,
    rets,
    sums,
    homes,
    hidden_ref,
    finals,
    core_sends,
    core_arrivals,
    meta_sends,
    meta_arrivals,
    block_sends,
    block_arrivals,
    pick_sends,
    pick_arrivals,
    ret_sends,
    ret_arrivals,
    home_sends,
    home_arrivals,
):
    section = lax.axis_index("section")
    me = lax.axis_index("expert")
    level = me // 4
    plane = lax.rem(me, 4)
    x_at = lax.rem(plane, 2)
    y_at = plane // 2
    rows, width = hidden_ref.shape
    groups = 4 * depth

    def at_level(offset):
        return lax.rem(level + offset + depth, depth) * 4 + plane

    def beside(j):
        x_to = 1 - x_at if j % 2 else x_at
        y_to = 1 - y_at if j // 2 else y_at
        return y_to * 2 + x_to

    def in_plane(j):
        return level * 4 + beside(j)

    barrier = pltpu.get_barrier_semaphore()
    partners = [{"section": 1 - section}]
    partners += [{"expert": at_level(k)} for k in range(1, depth)]
    partners += [{"expert": in_plane(j)} for j in range(1, 4)]
    for partner in partners:
        pl.semaphore_signal(
            barrier, inc=1, device_id=partner, device_id_type=pl.DeviceIdType.MESH
        )
    pl.semaphore_wait(barrier, len(partners))

    started = []

    def send(source, target, send_sem, arrival_sem, **peer):
        copy = pltpu.make_async_remote_copy(
            src_ref=source,
            dst_ref=target,
            send_sem=send_sem,
            recv_sem=arrival_sem,
            device_id=peer,
            device_id_type=pl.DeviceIdType.MESH,
        )
        copy.start()
        started.append(copy)
        return copy

    def to_core(i, source, target):
        return send(source, target, core_sends.at[i], core_arrivals.at[i], section=1 - section)

    gain_copy = to_core(0, gain_ref, other_gain)
    dense_copy = to_core(1, dense_ref.at[1 - section], other_dense)
    mats = [(gate_hbm, gate_mats), (up_hbm, up_mats), (down_hbm, down_mats)]
    mat_copies = [
        to_core(2 + i, source, target.at[section]) for i, (source, target) in enumerate(mats)
    ]
    own_copies = [
        pltpu.make_async_copy(source, target.at[section], core_sends.at[6 + i])
        for i, (source, target) in enumerate(mats)
    ]
    for copy in own_copies:
        copy.start()

    hidden_ref[...] = tokens_ref[section].astype(jnp.float32)
    gain_copy.wait_recv()
    is_first = section == 0
    gains = [
        jnp.where(is_first, gain_ref[...], other_gain[...]),
        jnp.where(is_first, other_gain[...], gain_ref[...]),
    ]

    def normed(layer):
        values = hidden_ref[...]
        inverse_rms = lax.rsqrt(jnp.mean(values * values, axis=-1, keepdims=True) + EPSILON)
        return (values * inverse_rms * gains[layer]).astype(jnp.bfloat16)

    row_at = lax.broadcasted_iota(jnp.int32, (rows, rows), 0)
    col_at = lax.broadcasted_iota(jnp.int32, (rows, rows), 1)
    earlier = jnp.where(col_at < row_at, 1.0, 0.0).astype(jnp.bfloat16)
    lane_of = lax.broadcasted_iota(jnp.int32, (rows, 128), 1)
    key_row = lax.broadcasted_iota(jnp.int32, (8, 128), 0)
    key_lane = lax.broadcasted_iota(jnp.int32, (8, 128), 1)

    for layer in range(2):
        blocks[layer, 0] = normed(layer)
        by_z = [None] + [
            send(
                blocks.at[layer, 0],
                blocks.at[layer, k],
                block_sends.at[layer, k],
                block_arrivals.at[layer, k],
                expert=at_level(k),
            )
            for k in range(1, depth)
        ]
        if layer == 0:
            dense_copy.wait_recv()
            meta[0] = dense_ref[section] + other_dense[...]
            meta_copies = [None] + [
                send(
                    meta.at[0],
                    meta.at[k],
                    meta_sends.at[k],
                    meta_arrivals.at[k],
                    expert=at_level(k),
                )
                for k in range(1, depth)
            ]
        lanes = [layer * groups + level * 4 + beside(j) for j in range(4)]
        picked, returned, homeward = {}, {}, {}

        def slots(k):
            chosen = meta[k] > 0.0
            flags = jnp.where(chosen, 1.0, 0.0).astype(jnp.bfloat16)
            before = jnp.dot(earlier, flags, preferred_element_type=jnp.float32)
            return jnp.where(chosen, before, -512.0)

        def select(k):
            if k:
                by_z[k].wait_recv()
                if layer == 0:
                    meta_copies[k].wait_recv()
            keys = jnp.zeros((8, 128), jnp.float32)
            for j in range(4):
                keys = jnp.where((key_row == j) & (key_lane == lanes[j]), 1.0, keys)
            across = lax.dot_general(
                keys.astype(jnp.bfloat16),
                slots(k).astype(jnp.bfloat16),
                (((1,), (1,)), ((), ())),
                preferred_element_type=jnp.float32,
            )
            slot_at = lax.broadcasted_iota(jnp.int32, (4 * cap, rows), 0).astype(jnp.float32)
            hits = jnp.zeros((4 * cap, rows), jnp.float32)
            for j in range(4):
                hits = jnp.where(slot_at == across[j : j + 1, :] + float(j * cap), 1.0, hits)
            taken = jnp.dot(
                hits.astype(jnp.bfloat16), blocks[layer, k], preferred_element_type=jnp.float32
            ).astype(jnp.bfloat16)
            for j in range(1, 4):
                picks[layer, k, j] = taken[j * cap : (j + 1) * cap]
                picked[k, j] = send(
                    picks.at[layer, k, j],
                    held.at[layer, k, j],
                    pick_sends.at[layer, k, j],
                    pick_arrivals.at[layer, k, j],
                    expert=in_plane(j),
                )
            held[layer, k, 0] = taken[0:cap]

        def compute(k):
            for j in range(1, 4):
                picked[k, j].wait_recv()
            block = held[layer, k].reshape(4 * cap, width)
            gate_part = jnp.dot(block, gate_mats[layer], preferred_element_type=jnp.float32)
            up_part = jnp.dot(block, up_mats[layer], preferred_element_type=jnp.float32)
            hidden_units = (gate_part / (1.0 + jnp.exp(-gate_part)) * up_part).astype(
                jnp.bfloat16
            )
            out = jnp.dot(hidden_units, down_mats[layer], preferred_element_type=jnp.float32)
            out = out.astype(jnp.bfloat16)
            for j in range(1, 4):
                outs[layer, k, j] = out[j * cap : (j + 1) * cap]
                returned[k, j] = send(
                    outs.at[layer, k, j],
                    rets.at[layer, k, j],
                    ret_sends.at[layer, k, j],
                    ret_arrivals.at[layer, k, j],
                    expert=in_plane(j),
                )
            rets[layer, k, 0] = out[0:cap]

        def combine(k):
            for j in range(1, 4):
                returned[k, j].wait_recv()
            place = slots(k)
            weights = meta[k]
            slot_at = lax.broadcasted_iota(jnp.int32, (rows, 4 * cap), 1).astype(jnp.float32)
            spread = jnp.zeros((rows, 4 * cap), jnp.float32)
            for j in range(4):
                named = lane_of == lanes[j]
                slot = jnp.sum(jnp.where(named, place, 0.0), axis=1, keepdims=True)
                weight = jnp.sum(jnp.where(named, weights, 0.0), axis=1, keepdims=True)
                spread = jnp.where(slot_at == slot + float(j * cap), weight, spread)
            high = spread.astype(jnp.bfloat16)
            low = (spread - high.astype(jnp.float32)).astype(jnp.bfloat16)
            both = jnp.dot(
                jnp.concatenate([high, low], axis=0),
                rets[layer, k].reshape(4 * cap, width),
                preferred_element_type=jnp.float32,
            )
            return both[0:rows] + both[rows:]

        def combine_home(k):
            sums[layer, k] = combine(k).astype(jnp.bfloat16)
            homeward[k] = send(
                sums.at[layer, k],
                homes.at[layer, k],
                home_sends.at[layer, k],
                home_arrivals.at[layer, k],
                expert=at_level(-k),
            )

        for k in range(depth):
            select(k)
        if layer == 0:
            for copy in own_copies:
                copy.wait()
            for copy in mat_copies:
                copy.wait_recv()
        for k in range(1, depth):
            compute(k)
        compute(0)
        for k in range(1, depth):
            combine_home(k)
        mixture = combine(0)
        for k in range(1, depth):
            homeward[k].wait_recv()
            mixture = mixture + homes[layer, k].astype(jnp.float32)
        hidden = (hidden_ref[...] + mixture).astype(jnp.bfloat16)
        if layer == 0:
            hidden_ref[...] = hidden.astype(jnp.float32)
        else:
            finals[0] = hidden

    final_copy = to_core(5, finals.at[0], finals.at[1])
    out_ref[section] = finals[0]
    final_copy.wait_recv()
    out_ref[1 - section] = finals[1]
    for copy in started:
        copy.wait_send()


def cascade_call(tokens, gain, dense, gate_matrix, up_matrix, down_matrix, depth, cap):
    rows, width = tokens.shape[1:]
    vmem = pl.BlockSpec(memory_space=pltpu.VMEM)
    anywhere = pl.BlockSpec(memory_space=pl.ANY)
    bf16, f32 = jnp.bfloat16, jnp.float32
    sems = pltpu.SemaphoreType.DMA
    return pl.pallas_call(
        functools.partial(cascade_kernel, depth, cap),
        out_shape=jax.ShapeDtypeStruct((2, rows, width), bf16),
        in_specs=[vmem, vmem, vmem, anywhere, anywhere, anywhere],
        out_specs=vmem,
        scratch_shapes=[
            pltpu.VMEM((2,) + gate_matrix.shape, bf16),
            pltpu.VMEM((2,) + up_matrix.shape, bf16),
            pltpu.VMEM((2,) + down_matrix.shape, bf16),
            pltpu.VMEM(gain.shape, f32),
            pltpu.VMEM(dense.shape[1:], f32),
            pltpu.VMEM((depth,) + dense.shape[1:], f32),
            pltpu.VMEM((2, depth, rows, width), bf16),
            pltpu.VMEM((2, depth, 4, cap, width), bf16),
            pltpu.VMEM((2, depth, 4, cap, width), bf16),
            pltpu.VMEM((2, depth, 4, cap, width), bf16),
            pltpu.VMEM((2, depth, 4, cap, width), bf16),
            pltpu.VMEM((2, depth, rows, width), bf16),
            pltpu.VMEM((2, depth, rows, width), bf16),
            pltpu.VMEM((rows, width), f32),
            pltpu.VMEM((2, rows, width), bf16),
            sems((9,)),
            sems((6,)),
            sems((depth,)),
            sems((depth,)),
            sems((2, depth)),
            sems((2, depth)),
            sems((2, depth, 4)),
            sems((2, depth, 4)),
            sems((2, depth, 4)),
            sems((2, depth, 4)),
            sems((2, depth)),
            sems((2, depth)),
        ],
        compiler_params=pltpu.CompilerParams(
            collective_id=0,
            has_side_effects=True,
            vmem_limit_bytes=60 * 1024 * 1024,
        ),
    )(tokens, gain, dense, gate_matrix, up_matrix, down_matrix)


def dense_local(
    tokens, norm_gain, gate_weight, up_weight, down_weight, expert_place, expert_ids, route_weights
):
    groups = lax.axis_size("expert")
    section_index = lax.axis_index("section")
    tok_rows, top_count = expert_ids.shape[2:]
    cap = 5 * tok_rows * top_count // (4 * groups)
    experts = jnp.arange(groups, dtype=jnp.int32)
    held_by = jnp.sum(
        jnp.where(expert_ids[0][..., None] == experts, expert_place[0], 0), axis=-1
    )
    lanes = jnp.arange(128, dtype=jnp.int32) - groups * section_index
    dense = jnp.sum(
        jnp.where(held_by[..., None] == lanes, route_weights[0][..., None], 0.0), axis=2
    )
    return cascade_call(
        tokens,
        norm_gain,
        dense,
        gate_weight[0, 0],
        up_weight[0, 0],
        down_weight[0, 0],
        groups // 4,
        cap,
    )


def local(
    tokens, norm_gain, gate_weight, up_weight, down_weight, expert_place, expert_ids, route_weights
):
    dense = 2 * expert_ids.shape[3] >= expert_place.shape[1] and tokens.shape[0] == 2
    dense = dense and lax.axis_size("expert") % 4 == 0 and 4 < lax.axis_size("expert") <= 64
    run = dense_local if dense else routed_local
    return run(
        tokens,
        norm_gain,
        gate_weight,
        up_weight,
        down_weight,
        expert_place,
        expert_ids,
        route_weights,
    )


def solution(mesh):
    in_specs = (
        P(None, "expert", None),
        P("section", None),
        P("section", "expert", None, None),
        P("section", "expert", None, None),
        P("section", "expert", None, None),
        P("section", None),
        P("section", None, "expert", None),
        P("section", None, "expert", None),
    )
    out_specs = P(None, "expert", None)
    return jax.shard_map(local, mesh=mesh, in_specs=in_specs, out_specs=out_specs, check_vma=False)
```

time: 201 us -> 167 us (0.83)
  Pallas kernels: 189 us -> 162 us
  other arithmetic: 7.25 us -> 1.8 us
  blocking collectives: 2.39 us -> 0 us
    pallas_call x2 -> x1, Pallas kernels: 189 us -> 162 us  [cascade_call(): pl.pallas_call(functools.partial(cascade_kernel, depth, cap), out_shape=j...]
    all_gather x1 -> x0, blocking collectives: 2.39 us -> none  [dense_local(): return lax.all_gather(hidden[None], 'section', axis=0, tiled=True)]
    reduce_sum x3 -> x1, other arithmetic: 3.02 us -> 0.81 us  [dense_local(): jnp.sum(jnp.where(expert_ids[0][..., None] == experts, expert_place[0], 0...]
  transfers between devices with their start and end apart: 2 -> 0, of which waited for: 0 -> 0; matrix products, arithmetic and copies ran while one was open for 1% -> 0% of each run, Pallas kernels for 0% -> 0%
where the time goes in v1:
time: 167 us
  Pallas kernels  162 us (97%)
  local copies, waits for them, and re-layouts  2.76 us (2%)
  other arithmetic  1.8 us (1%)
    pallas_call x1, Pallas kernels, cascade_call(): pl.pallas_call(functools.partial(cascade_kernel, depth, cap), out_shape=j...  162 us

profile of v1, /device:TPU:0, one launch (start us, length us, event | category | flops | bytes accessed | tf_op | source)
XLA Modules:
  0.0 166.5 jit_solution(4975069146141849686)
XLA Ops:
  0.0 0.8 select_reduce_fusion.1
  0.8 0.1 copy.11
  0.9 0.8 copy.12
  1.7 1.0 select_reduce_fusion.dense_ref
  2.7 161.9 %shard_map.82 = bf16[2,64,2048]{2,1,0:T(8,128)(2,1)} custom-call(bf16[2,64,2048]{2,1,0:T(8,128)(2,1)} %tokens_ref.1, f32[1,2048]{1,0:T(1,128)} %gain_ref.1, f32[2,64,128]{2,1,0:T(8,128)} %select_reduce_fusion.dense_ref, bf16[2048,768]{1,0:T(8,128)(2,1)} %bitcast.6, bf16[2048,768]{1,0:T(8,128)(2,1)} %bitcast.7, bf16[768,2048]{1,0:T(8,128)(2,1)} %bitcast.8), custom_call_target="tpu_custom_call" | custom-call | tf_op jit(solution)/shard_map/pallas_call | solution.py:396
  164.6 1.9 %copy.14 = bf16[2,64,2048]{2,1,0:T(8,128)(2,1)} copy(bf16[2,64,2048]{2,1,0:T(8,128)(2,1)} %shard_map.82) | data formatting | bytes 1048576
  (1 shorter events, 0.0 us)

commit v2 on v1

--- a/solution.py
+++ b/solution.py
@@ -135,12 +135,14 @@
     other_gain,
     other_dense,
     meta,
+    places,
     blocks,
     picks,
     held,
     outs,
     rets,
     sums,
+    relays,
     homes,
     hidden_ref,
     finals,
@@ -156,6 +158,7 @@
     ret_arrivals,
     home_sends,
     home_arrivals,
+    relay_arrivals,
 ):
     section = lax.axis_index("section")
     me = lax.axis_index("expert")
@@ -164,10 +167,14 @@
     x_at = lax.rem(plane, 2)
     y_at = plane // 2
     rows, width = hidden_ref.shape
-    groups = 4 * depth
-
-    def at_level(offset):
-        return lax.rem(level + offset + depth, depth) * 4 + plane
+    upper = level // 2
+    outer = jnp.where(upper == 1, lax.rem(level, 2), 1 - lax.rem(level, 2))
+    mate = level + 1 - 2 * lax.rem(level, 2)
+    far_inner = 2 - upper
+    far_outer = 3 - 3 * upper
+
+    def at_level(z):
+        return z * 4 + plane
 
     def beside(j):
         x_to = 1 - x_at if j % 2 else x_at
@@ -179,7 +186,7 @@
 
     barrier = pltpu.get_barrier_semaphore()
     partners = [{"section": 1 - section}]
-    partners += [{"expert": at_level(k)} for k in range(1, depth)]
+    partners += [{"expert": at_level(z)} for z in (mate, far_inner, far_outer)]
     partners += [{"expert": in_plane(j)} for j in range(1, 4)]
     for partner in partners:
         pl.semaphore_signal(
@@ -187,10 +194,10 @@
         )
     pl.semaphore_wait(barrier, len(partners))
 
-    started = []
-
-    def send(source, target, send_sem, arrival_sem, **peer):
-        copy = pltpu.make_async_remote_copy(
+    started, inner_only = [], []
+
+    def remote(source, target, send_sem, arrival_sem, **peer):
+        return pltpu.make_async_remote_copy(
             src_ref=source,
             dst_ref=target,
             send_sem=send_sem,
@@ -198,9 +205,15 @@
             device_id=peer,
             device_id_type=pl.DeviceIdType.MESH,
         )
+
+    def send(*ends, **peer):
+        copy = remote(*ends, **peer)
         copy.start()
         started.append(copy)
         return copy
+
+    def wait_for(target, arrival_sem):
+        remote(target, target, arrival_sem, arrival_sem, expert=at_level(mate)).wait_recv()
 
     def to_core(i, source, target):
         return send(source, target, core_sends.at[i], core_arrivals.at[i], section=1 - section)
@@ -219,6 +232,14 @@
         copy.start()
 
     hidden_ref[...] = tokens_ref[section].astype(jnp.float32)
+    dense_copy.wait_recv()
+    meta[0] = dense_ref[section] + other_dense[...]
+    meta_copies = [
+        send(meta.at[0], meta.at[slot], meta_sends.at[i], meta_arrivals.at[slot], expert=at_level(z))
+        for i, (z, slot) in enumerate(
+            [(mate, 1), (far_inner, 2 + outer), (far_outer, 2 + outer)]
+        )
+    ]
     gain_copy.wait_recv()
     is_first = section == 0
     gains = [
@@ -231,67 +252,62 @@
         inverse_rms = lax.rsqrt(jnp.mean(values * values, axis=-1, keepdims=True) + EPSILON)
         return (values * inverse_rms * gains[layer]).astype(jnp.bfloat16)
 
-    row_at = lax.broadcasted_iota(jnp.int32, (rows, rows), 0)
-    col_at = lax.broadcasted_iota(jnp.int32, (rows, rows), 1)
-    earlier = jnp.where(col_at < row_at, 1.0, 0.0).astype(jnp.bfloat16)
-    lane_of = lax.broadcasted_iota(jnp.int32, (rows, 128), 1)
-    key_row = lax.broadcasted_iota(jnp.int32, (8, 128), 0)
-    key_lane = lax.broadcasted_iota(jnp.int32, (8, 128), 1)
+    span = meta.shape[2]
+    row_at = lax.broadcasted_iota(jnp.int32, (span, span), 0)
+    col_at = lax.broadcasted_iota(jnp.int32, (span, span), 1)
+    earlier = jnp.where(row_at < col_at, 1.0, 0.0).astype(jnp.bfloat16)
+    slot_at = lax.broadcasted_iota(jnp.int32, (4 * cap, rows), 0).astype(jnp.float32)
+
+    def place_slots(k):
+        chosen = meta[k] > 0.0
+        flags = jnp.where(chosen, 1.0, 0.0).astype(jnp.bfloat16)
+        before = jnp.dot(flags, earlier, preferred_element_type=jnp.float32)
+        places[k] = jnp.where(chosen, before, -512.0)
+
+    def spread_over(k, layer, weighted):
+        spread = jnp.zeros((4 * cap, rows), jnp.float32)
+        for j in range(4):
+            row = pl.ds(layer * 4 * depth + in_plane(j), 1)
+            slot = places[k, row, 0:rows]
+            value = meta[k, row, 0:rows] if weighted else 1.0
+            spread = jnp.where(slot_at == slot + float(j * cap), value, spread)
+        return spread
 
     for layer in range(2):
         blocks[layer, 0] = normed(layer)
-        by_z = [None] + [
-            send(
-                blocks.at[layer, 0],
-                blocks.at[layer, k],
-                block_sends.at[layer, k],
-                block_arrivals.at[layer, k],
-                expert=at_level(k),
+
+        def block_copy(i, source, slot, z):
+            return remote(
+                blocks.at[layer, source],
+                blocks.at[layer, slot],
+                block_sends.at[layer, i],
+                block_arrivals.at[layer, slot],
+                expert=at_level(z),
             )
-            for k in range(1, depth)
-        ]
-        if layer == 0:
-            dense_copy.wait_recv()
-            meta[0] = dense_ref[section] + other_dense[...]
-            meta_copies = [None] + [
-                send(
-                    meta.at[0],
-                    meta.at[k],
-                    meta_sends.at[k],
-                    meta_arrivals.at[k],
-                    expert=at_level(k),
-                )
-                for k in range(1, depth)
-            ]
-        lanes = [layer * groups + level * 4 + beside(j) for j in range(4)]
-        picked, returned, homeward = {}, {}, {}
-
-        def slots(k):
-            chosen = meta[k] > 0.0
-            flags = jnp.where(chosen, 1.0, 0.0).astype(jnp.bfloat16)
-            before = jnp.dot(earlier, flags, preferred_element_type=jnp.float32)
-            return jnp.where(chosen, before, -512.0)
+
+        for copy in (block_copy(0, 0, 1, mate), block_copy(1, 0, 2 + outer, far_inner)):
+            copy.start()
+            started.append(copy)
+        picked, returned = {}, {}
+
+        def block_arrived(k):
+            wait_for(blocks.at[layer, k], block_arrivals.at[layer, k])
+            if k >= 2:
+                forward = block_copy(k, k, k, mate)
+                inner_only.append(forward)
+                pl.when(outer == 0)(forward.start)
 
         def select(k):
+            if layer == 0:
+                if k:
+                    wait_for(meta.at[k], meta_arrivals.at[k])
+                place_slots(k)
             if k:
-                by_z[k].wait_recv()
-                if layer == 0:
-                    meta_copies[k].wait_recv()
-            keys = jnp.zeros((8, 128), jnp.float32)
-            for j in range(4):
-                keys = jnp.where((key_row == j) & (key_lane == lanes[j]), 1.0, keys)
-            across = lax.dot_general(
-                keys.astype(jnp.bfloat16),
-                slots(k).astype(jnp.bfloat16),
-                (((1,), (1,)), ((), ())),
+                block_arrived(k)
+            taken = jnp.dot(
+                spread_over(k, layer, False).astype(jnp.bfloat16),
+                blocks[layer, k],
                 preferred_element_type=jnp.float32,
-            )
-            slot_at = lax.broadcasted_iota(jnp.int32, (4 * cap, rows), 0).astype(jnp.float32)
-            hits = jnp.zeros((4 * cap, rows), jnp.float32)
-            for j in range(4):
-                hits = jnp.where(slot_at == across[j : j + 1, :] + float(j * cap), 1.0, hits)
-            taken = jnp.dot(
-                hits.astype(jnp.bfloat16), blocks[layer, k], preferred_element_type=jnp.float32
             ).astype(jnp.bfloat16)
             for j in range(1, 4):
                 picks[layer, k, j] = taken[j * cap : (j + 1) * cap]
@@ -329,33 +345,40 @@
         def combine(k):
             for j in range(1, 4):
                 returned[k, j].wait_recv()
-            place = slots(k)
-            weights = meta[k]
-            slot_at = lax.broadcasted_iota(jnp.int32, (rows, 4 * cap), 1).astype(jnp.float32)
-            spread = jnp.zeros((rows, 4 * cap), jnp.float32)
-            for j in range(4):
-                named = lane_of == lanes[j]
-                slot = jnp.sum(jnp.where(named, place, 0.0), axis=1, keepdims=True)
-                weight = jnp.sum(jnp.where(named, weights, 0.0), axis=1, keepdims=True)
-                spread = jnp.where(slot_at == slot + float(j * cap), weight, spread)
+            spread = spread_over(k, layer, True)
             high = spread.astype(jnp.bfloat16)
             low = (spread - high.astype(jnp.float32)).astype(jnp.bfloat16)
-            both = jnp.dot(
-                jnp.concatenate([high, low], axis=0),
+            both = lax.dot_general(
+                jnp.concatenate([high, low], axis=1),
                 rets[layer, k].reshape(4 * cap, width),
+                (((0,), (0,)), ((), ())),
                 preferred_element_type=jnp.float32,
             )
             return both[0:rows] + both[rows:]
 
-        def combine_home(k):
-            sums[layer, k] = combine(k).astype(jnp.bfloat16)
-            homeward[k] = send(
-                sums.at[layer, k],
-                homes.at[layer, k],
-                home_sends.at[layer, k],
-                home_arrivals.at[layer, k],
-                expert=at_level(-k),
+        def send_home(k, target, arrival, z):
+            copy = remote(
+                sums.at[layer, k], target, home_sends.at[layer, k], arrival, expert=at_level(z)
             )
+            copy.start()
+            return copy
+
+        def combine_far(k):
+            part = combine(k)
+            relay, arrival = relays.at[layer, k - 2], relay_arrivals.at[layer, k - 2]
+
+            @pl.when(outer == 1)
+            def _():
+                sums[layer, k] = part.astype(jnp.bfloat16)
+                send_home(k, relay, arrival, mate)
+
+            @pl.when(outer == 0)
+            def _():
+                wait_for(relay, arrival)
+                joined = part + relays[layer, k - 2].astype(jnp.float32)
+                sums[layer, k] = joined.astype(jnp.bfloat16)
+                z = far_inner if k == 2 else far_outer
+                send_home(k, homes.at[layer, 1], home_arrivals.at[layer, 1], z)
 
         for k in range(depth):
             select(k)
@@ -364,15 +387,16 @@
                 copy.wait()
             for copy in mat_copies:
                 copy.wait_recv()
-        for k in range(1, depth):
+        for k in (2, 3, 1, 0):
             compute(k)
-        compute(0)
-        for k in range(1, depth):
-            combine_home(k)
+        combine_far(2)
+        combine_far(3)
+        sums[layer, 1] = combine(1).astype(jnp.bfloat16)
+        started.append(send_home(1, homes.at[layer, 0], home_arrivals.at[layer, 0], mate))
         mixture = combine(0)
-        for k in range(1, depth):
-            homeward[k].wait_recv()
-            mixture = mixture + homes[layer, k].astype(jnp.float32)
+        for i in range(2):
+            wait_for(homes.at[layer, i], home_arrivals.at[layer, i])
+            mixture = mixture + homes[layer, i].astype(jnp.float32)
         hidden = (hidden_ref[...] + mixture).astype(jnp.bfloat16)
         if layer == 0:
             hidden_ref[...] = hidden.astype(jnp.float32)
@@ -383,8 +407,17 @@
     out_ref[section] = finals[0]
     final_copy.wait_recv()
     out_ref[1 - section] = finals[1]
+    for layer in range(2):
+        for k in (2, 3):
+            done = home_sends.at[layer, k]
+            started.append(remote(sums.at[layer, k], sums.at[layer, k], done, done, expert=at_level(mate)))
     for copy in started:
         copy.wait_send()
+
+    @pl.when(outer == 0)
+    def _():
+        for copy in inner_only:
+            copy.wait_send()
 
 
 def cascade_call(tokens, gain, dense, gate_matrix, up_matrix, down_matrix, depth, cap):
@@ -405,13 +438,15 @@
             pltpu.VMEM(gain.shape, f32),
             pltpu.VMEM(dense.shape[1:], f32),
             pltpu.VMEM((depth,) + dense.shape[1:], f32),
+            pltpu.VMEM((depth,) + dense.shape[1:], f32),
             pltpu.VMEM((2, depth, rows, width), bf16),
             pltpu.VMEM((2, depth, 4, cap, width), bf16),
             pltpu.VMEM((2, depth, 4, cap, width), bf16),
             pltpu.VMEM((2, depth, 4, cap, width), bf16),
             pltpu.VMEM((2, depth, 4, cap, width), bf16),
             pltpu.VMEM((2, depth, rows, width), bf16),
-            pltpu.VMEM((2, depth, rows, width), bf16),
+            pltpu.VMEM((2, 2, rows, width), bf16),
+            pltpu.VMEM((2, 2, rows, width), bf16),
             pltpu.VMEM((rows, width), f32),
             pltpu.VMEM((2, rows, width), bf16),
             sems((9,)),
@@ -425,7 +460,8 @@
             sems((2, depth, 4)),
             sems((2, depth, 4)),
             sems((2, depth)),
-            sems((2, depth)),
+            sems((2, 2)),
+            sems((2, 2)),
         ],
         compiler_params=pltpu.CompilerParams(
             collective_id=0,
@@ -446,10 +482,14 @@
     held_by = jnp.sum(
         jnp.where(expert_ids[0][..., None] == experts, expert_place[0], 0), axis=-1
     )
-    lanes = jnp.arange(128, dtype=jnp.int32) - groups * section_index
+    holders = jnp.arange(2 * groups, dtype=jnp.int32) - groups * section_index
     dense = jnp.sum(
-        jnp.where(held_by[..., None] == lanes, route_weights[0][..., None], 0.0), axis=2
-    )
+        jnp.where(
+            held_by[:, None] == holders[:, None, None], route_weights[0][:, None], 0.0
+        ),
+        axis=-1,
+    )
+    dense = jnp.pad(dense, ((0, 0), (0, 0), (0, -tok_rows % 128)))
     return cascade_call(
         tokens,
         norm_gain,
@@ -466,7 +506,7 @@
     tokens, norm_gain, gate_weight, up_weight, down_weight, expert_place, expert_ids, route_weights
 ):
     dense = 2 * expert_ids.shape[3] >= expert_place.shape[1] and tokens.shape[0] == 2
-    dense = dense and lax.axis_size("expert") % 4 == 0 and 4 < lax.axis_size("expert") <= 64
+    dense = dense and lax.axis_size("expert") % 4 == 0 and lax.axis_size("expert") == 16
     run = dense_local if dense else routed_local
     return run(
         tokens,

time: 167 us -> 146 us (0.87)
  Pallas kernels: 162 us -> 141 us
    pallas_call x1, Pallas kernels: 162 us -> 141 us  [cascade_call(): pl.pallas_call(functools.partial(cascade_kernel, depth, cap), out_shape=j...]
where the time goes in v2:
time: 146 us; the launch traced here: 145 us
  Pallas kernels  141 us (97%)
  local copies, waits for them, and re-layouts  2.5 us (2%)
  other arithmetic  1.67 us (1%)
    pallas_call x1, Pallas kernels, cascade_call(): pl.pallas_call(functools.partial(cascade_kernel, depth, cap), out_shape=j...  141 us

profile of v2, /device:TPU:0, one launch (start us, length us, event | category | flops | bytes accessed | tf_op | source)
XLA Modules:
  0.0 145.5 jit_solution(12896776411562729317)
XLA Ops:
  0.0 0.8 select_reduce_fusion.1
  0.8 0.9 select_reduce_fusion
  1.7 0.6 pad.4.dense_ref
  2.3 141.3 %shard_map.82 = bf16[2,64,2048]{2,1,0:T(8,128)(2,1)} custom-call(bf16[2,64,2048]{2,1,0:T(8,128)(2,1)} %tokens_ref.1, f32[1,2048]{1,0:T(1,128)} %gain_ref.1, f32[2,32,128]{2,1,0:T(8,128)} %pad.4.dense_ref, bf16[2048,768]{1,0:T(8,128)(2,1)} %bitcast.6, bf16[2048,768]{1,0:T(8,128)(2,1)} %bitcast.7, bf16[768,2048]{1,0:T(8,128)(2,1)} %bitcast.8), custom_call_target="tpu_custom_call" | custom-call | tf_op jit(solution)/shard_map/pallas_call | solution.py:429
  143.6 1.9 %copy.12 = bf16[2,64,2048]{2,1,0:T(8,128)(2,1)} copy(bf16[2,64,2048]{2,1,0:T(8,128)(2,1)} %shard_map.82) | data formatting | bytes 1048576
  (1 shorter events, 0.0 us)

commit v3 on v2

--- a/solution.py
+++ b/solution.py
@@ -144,6 +144,14 @@
     sums,
     relays,
     homes,
+    flats,
+    flat_picks,
+    flat_held,
+    flat_outs,
+    flat_rets,
+    flat_sums,
+    flat_homes,
+    parts,
     hidden_ref,
     finals,
     core_sends,
@@ -159,6 +167,14 @@
     home_sends,
     home_arrivals,
     relay_arrivals,
+    flat_sends,
+    flat_arrivals,
+    flat_pick_sends,
+    flat_pick_arrivals,
+    flat_ret_sends,
+    flat_ret_arrivals,
+    flat_home_sends,
+    flat_home_arrivals,
 ):
     section = lax.axis_index("section")
     me = lax.axis_index("expert")
@@ -167,6 +183,7 @@
     x_at = lax.rem(plane, 2)
     y_at = plane // 2
     rows, width = hidden_ref.shape
+    main = blocks.shape[3]
     upper = level // 2
     outer = jnp.where(upper == 1, lax.rem(level, 2), 1 - lax.rem(level, 2))
     mate = level + 1 - 2 * lax.rem(level, 2)
@@ -234,12 +251,18 @@
     hidden_ref[...] = tokens_ref[section].astype(jnp.float32)
     dense_copy.wait_recv()
     meta[0] = dense_ref[section] + other_dense[...]
-    meta_copies = [
+    z_slots = [(mate, 1), (far_inner, 2 + outer), (far_outer, 2 + outer)]
+    for i, (z, slot) in enumerate(z_slots):
         send(meta.at[0], meta.at[slot], meta_sends.at[i], meta_arrivals.at[slot], expert=at_level(z))
-        for i, (z, slot) in enumerate(
-            [(mate, 1), (far_inner, 2 + outer), (far_outer, 2 + outer)]
+    for j in range(1, 4):
+        place = 3 + j
+        send(
+            meta.at[0],
+            meta.at[place],
+            meta_sends.at[place],
+            meta_arrivals.at[place],
+            expert=in_plane(j),
         )
-    ]
     gain_copy.wait_recv()
     is_first = section == 0
     gains = [
@@ -257,24 +280,49 @@
     col_at = lax.broadcasted_iota(jnp.int32, (span, span), 1)
     earlier = jnp.where(row_at < col_at, 1.0, 0.0).astype(jnp.bfloat16)
     slot_at = lax.broadcasted_iota(jnp.int32, (4 * cap, rows), 0).astype(jnp.float32)
-
-    def place_slots(k):
-        chosen = meta[k] > 0.0
+    plane_experts = [in_plane(j) for j in range(4)]
+    column_experts = [at_level(z) for z in (level, mate, far_inner, far_outer)]
+
+    def place_slots(place):
+        if place:
+            wait_for(meta.at[place], meta_arrivals.at[place])
+        chosen = meta[place] > 0.0
         flags = jnp.where(chosen, 1.0, 0.0).astype(jnp.bfloat16)
         before = jnp.dot(flags, earlier, preferred_element_type=jnp.float32)
-        places[k] = jnp.where(chosen, before, -512.0)
-
-    def spread_over(k, layer, weighted):
+        places[place] = jnp.where(chosen, before, -512.0)
+
+    def spread_over(place, experts, layer, weighted):
         spread = jnp.zeros((4 * cap, rows), jnp.float32)
-        for j in range(4):
-            row = pl.ds(layer * 4 * depth + in_plane(j), 1)
-            slot = places[k, row, 0:rows]
-            value = meta[k, row, 0:rows] if weighted else 1.0
+        for j, expert in enumerate(experts):
+            row = pl.ds(layer * 4 * depth + expert, 1)
+            slot = places[place, row, 0:rows]
+            value = meta[place, row, 0:rows] if weighted else 1.0
             spread = jnp.where(slot_at == slot + float(j * cap), value, spread)
         return spread
 
+    def take(place, experts, layer, block):
+        return jnp.dot(
+            spread_over(place, experts, layer, False).astype(jnp.bfloat16),
+            block,
+            preferred_element_type=jnp.float32,
+        ).astype(jnp.bfloat16)
+
+    def scatter(place, experts, layer, returned_rows):
+        spread = spread_over(place, experts, layer, True)
+        high = spread.astype(jnp.bfloat16)
+        low = (spread - high.astype(jnp.float32)).astype(jnp.bfloat16)
+        both = lax.dot_general(
+            jnp.concatenate([high, low], axis=1),
+            returned_rows.reshape(4 * cap, returned_rows.shape[-1]),
+            (((0,), (0,)), ((), ())),
+            preferred_element_type=jnp.float32,
+        )
+        return both[0:rows] + both[rows:]
+
     for layer in range(2):
-        blocks[layer, 0] = normed(layer)
+        start = normed(layer)
+        blocks[layer, 0] = start[:, 0:main]
+        flats[layer, 0] = start[:, main:]
 
         def block_copy(i, source, slot, z):
             return remote(
@@ -288,27 +336,39 @@
         for copy in (block_copy(0, 0, 1, mate), block_copy(1, 0, 2 + outer, far_inner)):
             copy.start()
             started.append(copy)
-        picked, returned = {}, {}
+        flat_copies = [None] + [
+            send(
+                flats.at[layer, 0],
+                flats.at[layer, j],
+                flat_sends.at[layer, j],
+                flat_arrivals.at[layer, j],
+                expert=in_plane(j),
+            )
+            for j in range(1, 4)
+        ]
+        picked, returned, flat_home = {}, {}, {}
 
         def block_arrived(k):
             wait_for(blocks.at[layer, k], block_arrivals.at[layer, k])
-            if k >= 2:
-                forward = block_copy(k, k, k, mate)
-                inner_only.append(forward)
-                pl.when(outer == 0)(forward.start)
+
+        def pass_on():
+            forwards = [block_copy(k, k, k, mate) for k in (2, 3)]
+            inner_only.extend(forwards)
+
+            @pl.when(outer == 0)
+            def _():
+                for k, forward in zip((2, 3), forwards):
+                    block_arrived(k)
+                    forward.start()
 
         def select(k):
             if layer == 0:
-                if k:
-                    wait_for(meta.at[k], meta_arrivals.at[k])
                 place_slots(k)
-            if k:
+            if k == 1:
                 block_arrived(k)
-            taken = jnp.dot(
-                spread_over(k, layer, False).astype(jnp.bfloat16),
-                blocks[layer, k],
-                preferred_element_type=jnp.float32,
-            ).astype(jnp.bfloat16)
+            if k >= 2:
+                pl.when(outer == 1)(functools.partial(block_arrived, k))
+            taken = take(k, plane_experts, layer, blocks[layer, k])
             for j in range(1, 4):
                 picks[layer, k, j] = taken[j * cap : (j + 1) * cap]
                 picked[k, j] = send(
@@ -320,19 +380,47 @@
                 )
             held[layer, k, 0] = taken[0:cap]
 
+        def select_flat(j):
+            place = 3 + j if j else 0
+            if j:
+                if layer == 0:
+                    place_slots(place)
+                flat_copies[j].wait_recv()
+            taken = take(place, column_experts, layer, flats[layer, j])
+            for i, (z, slot) in enumerate(z_slots):
+                flat_picks[layer, j, i] = taken[(i + 1) * cap : (i + 2) * cap]
+                send(
+                    flat_picks.at[layer, j, i],
+                    flat_held.at[layer, slot, j],
+                    flat_pick_sends.at[layer, j, i],
+                    flat_pick_arrivals.at[layer, slot, j],
+                    expert=at_level(z),
+                )
+            flat_held[layer, 0, j] = taken[0:cap]
+
         def compute(k):
             for j in range(1, 4):
                 picked[k, j].wait_recv()
-            block = held[layer, k].reshape(4 * cap, width)
-            gate_part = jnp.dot(block, gate_mats[layer], preferred_element_type=jnp.float32)
-            up_part = jnp.dot(block, up_mats[layer], preferred_element_type=jnp.float32)
+            if k:
+                for j in range(4):
+                    wait_for(flat_held.at[layer, k, j], flat_pick_arrivals.at[layer, k, j])
+            block = held[layer, k].reshape(4 * cap, main)
+            rest = flat_held[layer, k].reshape(4 * cap, width - main)
+
+            def project(mats):
+                return jnp.dot(
+                    block, mats[layer, 0:main], preferred_element_type=jnp.float32
+                ) + jnp.dot(rest, mats[layer, main:], preferred_element_type=jnp.float32)
+
+            gate_part = project(gate_mats)
+            up_part = project(up_mats)
             hidden_units = (gate_part / (1.0 + jnp.exp(-gate_part)) * up_part).astype(
                 jnp.bfloat16
             )
             out = jnp.dot(hidden_units, down_mats[layer], preferred_element_type=jnp.float32)
             out = out.astype(jnp.bfloat16)
             for j in range(1, 4):
-                outs[layer, k, j] = out[j * cap : (j + 1) * cap]
+                outs[layer, k, j] = out[j * cap : (j + 1) * cap, 0:main]
                 returned[k, j] = send(
                     outs.at[layer, k, j],
                     rets.at[layer, k, j],
@@ -340,21 +428,29 @@
                     ret_arrivals.at[layer, k, j],
                     expert=in_plane(j),
                 )
-            rets[layer, k, 0] = out[0:cap]
+            rets[layer, k, 0] = out[0:cap, 0:main]
+            flat_out = out[:, main:].reshape(4, cap, width - main)
+            if k:
+                flat_outs[layer, k - 1] = flat_out
+                z, slot = z_slots[k - 1]
+                send(
+                    flat_outs.at[layer, k - 1],
+                    flat_rets.at[layer, slot],
+                    flat_ret_sends.at[layer, k],
+                    flat_ret_arrivals.at[layer, slot],
+                    expert=at_level(z),
+                )
+            else:
+                flat_rets[layer, 0] = flat_out
 
         def combine(k):
             for j in range(1, 4):
                 returned[k, j].wait_recv()
-            spread = spread_over(k, layer, True)
-            high = spread.astype(jnp.bfloat16)
-            low = (spread - high.astype(jnp.float32)).astype(jnp.bfloat16)
-            both = lax.dot_general(
-                jnp.concatenate([high, low], axis=1),
-                rets[layer, k].reshape(4 * cap, width),
-                (((0,), (0,)), ((), ())),
-                preferred_element_type=jnp.float32,
-            )
-            return both[0:rows] + both[rows:]
+            return scatter(k, plane_experts, layer, rets[layer, k])
+
+        def combine_flat(j):
+            place = 3 + j if j else 0
+            return scatter(place, column_experts, layer, flat_rets[layer, :, j])
 
         def send_home(k, target, arrival, z):
             copy = remote(
@@ -365,23 +461,35 @@
 
         def combine_far(k):
             part = combine(k)
-            relay, arrival = relays.at[layer, k - 2], relay_arrivals.at[layer, k - 2]
 
             @pl.when(outer == 1)
             def _():
                 sums[layer, k] = part.astype(jnp.bfloat16)
+                relay, arrival = relays.at[layer, k - 2], relay_arrivals.at[layer, k - 2]
                 send_home(k, relay, arrival, mate)
 
             @pl.when(outer == 0)
             def _():
-                wait_for(relay, arrival)
-                joined = part + relays[layer, k - 2].astype(jnp.float32)
+                parts[k - 2] = part
+
+        def join_far(k):
+            @pl.when(outer == 0)
+            def _():
+                wait_for(relays.at[layer, k - 2], relay_arrivals.at[layer, k - 2])
+                joined = parts[k - 2] + relays[layer, k - 2].astype(jnp.float32)
                 sums[layer, k] = joined.astype(jnp.bfloat16)
                 z = far_inner if k == 2 else far_outer
                 send_home(k, homes.at[layer, 1], home_arrivals.at[layer, 1], z)
 
-        for k in range(depth):
-            select(k)
+        select(0)
+        select(1)
+        pass_on()
+        select(2)
+        select_flat(0)
+        select_flat(1)
+        select_flat(2)
+        select_flat(3)
+        select(3)
         if layer == 0:
             for copy in own_copies:
                 copy.wait()
@@ -393,11 +501,29 @@
         combine_far(3)
         sums[layer, 1] = combine(1).astype(jnp.bfloat16)
         started.append(send_home(1, homes.at[layer, 0], home_arrivals.at[layer, 0], mate))
+        for k in range(1, depth):
+            wait_for(flat_rets.at[layer, k], flat_ret_arrivals.at[layer, k])
+        for j in range(1, 4):
+            flat_sums[layer, j] = combine_flat(j).astype(jnp.bfloat16)
+            flat_home[j] = send(
+                flat_sums.at[layer, j],
+                flat_homes.at[layer, j],
+                flat_home_sends.at[layer, j],
+                flat_home_arrivals.at[layer, j],
+                expert=in_plane(j),
+            )
+        join_far(2)
+        flat_mixture = combine_flat(0)
+        join_far(3)
         mixture = combine(0)
+        for j in range(1, 4):
+            flat_home[j].wait_recv()
+            flat_mixture = flat_mixture + flat_homes[layer, j].astype(jnp.float32)
         for i in range(2):
             wait_for(homes.at[layer, i], home_arrivals.at[layer, i])
             mixture = mixture + homes[layer, i].astype(jnp.float32)
-        hidden = (hidden_ref[...] + mixture).astype(jnp.bfloat16)
+        mixed = jnp.concatenate([mixture, flat_mixture], axis=1)
+        hidden = (hidden_ref[...] + mixed).astype(jnp.bfloat16)
         if layer == 0:
             hidden_ref[...] = hidden.astype(jnp.float32)
         else:
@@ -422,6 +548,8 @@
 
 def cascade_call(tokens, gain, dense, gate_matrix, up_matrix, down_matrix, depth, cap):
     rows, width = tokens.shape[1:]
+    rest = width // 4 // 128 * 128
+    main = width - rest
     vmem = pl.BlockSpec(memory_space=pltpu.VMEM)
     anywhere = pl.BlockSpec(memory_space=pl.ANY)
     bf16, f32 = jnp.bfloat16, jnp.float32
@@ -437,22 +565,30 @@
             pltpu.VMEM((2,) + down_matrix.shape, bf16),
             pltpu.VMEM(gain.shape, f32),
             pltpu.VMEM(dense.shape[1:], f32),
-            pltpu.VMEM((depth,) + dense.shape[1:], f32),
-            pltpu.VMEM((depth,) + dense.shape[1:], f32),
-            pltpu.VMEM((2, depth, rows, width), bf16),
-            pltpu.VMEM((2, depth, 4, cap, width), bf16),
-            pltpu.VMEM((2, depth, 4, cap, width), bf16),
-            pltpu.VMEM((2, depth, 4, cap, width), bf16),
-            pltpu.VMEM((2, depth, 4, cap, width), bf16),
-            pltpu.VMEM((2, depth, rows, width), bf16),
-            pltpu.VMEM((2, 2, rows, width), bf16),
-            pltpu.VMEM((2, 2, rows, width), bf16),
+            pltpu.VMEM((depth + 3,) + dense.shape[1:], f32),
+            pltpu.VMEM((depth + 3,) + dense.shape[1:], f32),
+            pltpu.VMEM((2, depth, rows, main), bf16),
+            pltpu.VMEM((2, depth, 4, cap, main), bf16),
+            pltpu.VMEM((2, depth, 4, cap, main), bf16),
+            pltpu.VMEM((2, depth, 4, cap, main), bf16),
+            pltpu.VMEM((2, depth, 4, cap, main), bf16),
+            pltpu.VMEM((2, depth, rows, main), bf16),
+            pltpu.VMEM((2, 2, rows, main), bf16),
+            pltpu.VMEM((2, 2, rows, main), bf16),
+            pltpu.VMEM((2, 4, rows, rest), bf16),
+            pltpu.VMEM((2, 4, depth - 1, cap, rest), bf16),
+            pltpu.VMEM((2, depth, 4, cap, rest), bf16),
+            pltpu.VMEM((2, depth - 1, 4, cap, rest), bf16),
+            pltpu.VMEM((2, depth, 4, cap, rest), bf16),
+            pltpu.VMEM((2, 4, rows, rest), bf16),
+            pltpu.VMEM((2, 4, rows, rest), bf16),
+            pltpu.VMEM((2, rows, main), f32),
             pltpu.VMEM((rows, width), f32),
             pltpu.VMEM((2, rows, width), bf16),
             sems((9,)),
             sems((6,)),
-            sems((depth,)),
-            sems((depth,)),
+            sems((depth + 3,)),
+            sems((depth + 3,)),
             sems((2, depth)),
             sems((2, depth)),
             sems((2, depth, 4)),
@@ -462,6 +598,14 @@
             sems((2, depth)),
             sems((2, 2)),
             sems((2, 2)),
+            sems((2, 4)),
+            sems((2, 4)),
+            sems((2, 4, depth - 1)),
+            sems((2, depth, 4)),
+            sems((2, depth)),
+            sems((2, depth)),
+            sems((2, 4)),
+            sems((2, 4)),
         ],
         compiler_params=pltpu.CompilerParams(
             collective_id=0,

time: 146 us -> 129 us (0.88)
  Pallas kernels: 141 us -> 125 us
    pallas_call x1, Pallas kernels: 141 us -> 125 us  [cascade_call(): pl.pallas_call(functools.partial(cascade_kernel, depth, cap), out_shape=j...]
where the time goes in v3:
time: 129 us
  Pallas kernels  125 us (97%)
  local copies, waits for them, and re-layouts  2.5 us (2%)
  other arithmetic  1.67 us (1%)
    pallas_call x1, Pallas kernels, cascade_call(): pl.pallas_call(functools.partial(cascade_kernel, depth, cap), out_shape=j...  125 us

profile of v3, /device:TPU:0, one launch (start us, length us, event | category | flops | bytes accessed | tf_op | source)
XLA Modules:
  0.0 128.7 jit_solution(3914845370942713353)
XLA Ops:
  0.0 0.8 select_reduce_fusion.1
  0.8 0.9 select_reduce_fusion
  1.7 0.6 pad.4.dense_ref
  2.3 124.5 %shard_map.82 = bf16[2,64,2048]{2,1,0:T(8,128)(2,1)} custom-call(bf16[2,64,2048]{2,1,0:T(8,128)(2,1)} %tokens_ref.1, f32[1,2048]{1,0:T(1,128)} %gain_ref.1, f32[2,32,128]{2,1,0:T(8,128)} %pad.4.dense_ref, bf16[2048,768]{1,0:T(8,128)(2,1)} %bitcast.6, bf16[2048,768]{1,0:T(8,128)(2,1)} %bitcast.7, bf16[768,2048]{1,0:T(8,128)(2,1)} %bitcast.8), custom_call_target="tpu_custom_call" | custom-call | tf_op jit(solution)/shard_map/pallas_call | solution.py:557
  126.8 1.9 %copy.12 = bf16[2,64,2048]{2,1,0:T(8,128)(2,1)} copy(bf16[2,64,2048]{2,1,0:T(8,128)(2,1)} %shard_map.82) | data formatting | bytes 1048576
  (1 shorter events, 0.0 us)

commit v4 on v3

--- a/solution.py
+++ b/solution.py
@@ -124,11 +124,13 @@
     cap,
     tokens_ref,
     gain_ref,
-    dense_ref,
+    place_ref,
+    ids_ref,
+    route_ref,
     gate_hbm,
     up_hbm,
     down_hbm,
-    out_ref,
+    finals,
     gate_mats,
     up_mats,
     down_mats,
@@ -153,7 +155,7 @@
     flat_homes,
     parts,
     hidden_ref,
-    finals,
+    dense_ref,
     core_sends,
     core_arrivals,
     meta_sends,
@@ -183,7 +185,9 @@
     x_at = lax.rem(plane, 2)
     y_at = plane // 2
     rows, width = hidden_ref.shape
+    groups = 4 * depth
     main = blocks.shape[3]
+    back = outs.shape[4]
     upper = level // 2
     outer = jnp.where(upper == 1, lax.rem(level, 2), 1 - lax.rem(level, 2))
     mate = level + 1 - 2 * lax.rem(level, 2)
@@ -209,6 +213,29 @@
         pl.semaphore_signal(
             barrier, inc=1, device_id=partner, device_id_type=pl.DeviceIdType.MESH
         )
+
+    dense_ref[...] = jnp.zeros(dense_ref.shape, jnp.float32)
+    held_at = place_ref[...] + groups * section
+    holder_of = lax.broadcasted_iota(jnp.int32, (2 * groups, groups), 0)
+    moves = jnp.where(holder_of == held_at, 1.0, 0.0).astype(jnp.bfloat16)
+    expert_at = lax.broadcasted_iota(jnp.int32, (groups, rows), 0)
+    for m in range(2):
+        ids, route = ids_ref[m], route_ref[m]
+        named = jnp.zeros((groups, rows), jnp.float32)
+        for k in range(ids.shape[0]):
+            named = jnp.where(ids[k : k + 1] == expert_at, route[k : k + 1], named)
+        high = named.astype(jnp.bfloat16)
+        low = (named - high.astype(jnp.float32)).astype(jnp.bfloat16)
+        dense_ref[m, :, 0:rows] = sum(
+            jnp.dot(moves, part, preferred_element_type=jnp.float32) for part in (high, low)
+        )
+
+    def scaled():
+        values = hidden_ref[...]
+        return values * lax.rsqrt(jnp.mean(values * values, axis=-1, keepdims=True) + EPSILON)
+
+    hidden_ref[...] = tokens_ref[section].astype(jnp.float32)
+    first_scaled = scaled()
     pl.semaphore_wait(barrier, len(partners))
 
     started, inner_only = [], []
@@ -248,7 +275,6 @@
     for copy in own_copies:
         copy.start()
 
-    hidden_ref[...] = tokens_ref[section].astype(jnp.float32)
     dense_copy.wait_recv()
     meta[0] = dense_ref[section] + other_dense[...]
     z_slots = [(mate, 1), (far_inner, 2 + outer), (far_outer, 2 + outer)]
@@ -270,11 +296,6 @@
         jnp.where(is_first, other_gain[...], gain_ref[...]),
     ]
 
-    def normed(layer):
-        values = hidden_ref[...]
-        inverse_rms = lax.rsqrt(jnp.mean(values * values, axis=-1, keepdims=True) + EPSILON)
-        return (values * inverse_rms * gains[layer]).astype(jnp.bfloat16)
-
     span = meta.shape[2]
     row_at = lax.broadcasted_iota(jnp.int32, (span, span), 0)
     col_at = lax.broadcasted_iota(jnp.int32, (span, span), 1)
@@ -320,7 +341,8 @@
         return both[0:rows] + both[rows:]
 
     for layer in range(2):
-        start = normed(layer)
+        start = first_scaled if layer == 0 else scaled()
+        start = (start * gains[layer]).astype(jnp.bfloat16)
         blocks[layer, 0] = start[:, 0:main]
         flats[layer, 0] = start[:, main:]
 
@@ -420,7 +442,7 @@
             out = jnp.dot(hidden_units, down_mats[layer], preferred_element_type=jnp.float32)
             out = out.astype(jnp.bfloat16)
             for j in range(1, 4):
-                outs[layer, k, j] = out[j * cap : (j + 1) * cap, 0:main]
+                outs[layer, k, j] = out[j * cap : (j + 1) * cap, 0:back]
                 returned[k, j] = send(
                     outs.at[layer, k, j],
                     rets.at[layer, k, j],
@@ -428,8 +450,8 @@
                     ret_arrivals.at[layer, k, j],
                     expert=in_plane(j),
                 )
-            rets[layer, k, 0] = out[0:cap, 0:main]
-            flat_out = out[:, main:].reshape(4, cap, width - main)
+            rets[layer, k, 0] = out[0:cap, 0:back]
+            flat_out = out[:, back:].reshape(4, cap, width - back)
             if k:
                 flat_outs[layer, k - 1] = flat_out
                 z, slot = z_slots[k - 1]
@@ -530,9 +552,7 @@
             finals[0] = hidden
 
     final_copy = to_core(5, finals.at[0], finals.at[1])
-    out_ref[section] = finals[0]
     final_copy.wait_recv()
-    out_ref[1 - section] = finals[1]
     for layer in range(2):
         for k in (2, 3):
             done = home_sends.at[layer, k]
@@ -546,10 +566,13 @@
             copy.wait_send()
 
 
-def cascade_call(tokens, gain, dense, gate_matrix, up_matrix, down_matrix, depth, cap):
+def cascade_call(
+    tokens, gain, place, ids, route, gate_matrix, up_matrix, down_matrix, depth, cap
+):
     rows, width = tokens.shape[1:]
-    rest = width // 4 // 128 * 128
-    main = width - rest
+    table = (8 * depth, rows + -rows % 128)
+    main = width - width // 4 // 128 * 128
+    back = width - 3 * width // 16 // 128 * 128
     vmem = pl.BlockSpec(memory_space=pltpu.VMEM)
     anywhere = pl.BlockSpec(memory_space=pl.ANY)
     bf16, f32 = jnp.bfloat16, jnp.float32
@@ -557,34 +580,34 @@
     return pl.pallas_call(
         functools.partial(cascade_kernel, depth, cap),
         out_shape=jax.ShapeDtypeStruct((2, rows, width), bf16),
-        in_specs=[vmem, vmem, vmem, anywhere, anywhere, anywhere],
+        in_specs=[vmem] * 5 + [anywhere] * 3,
         out_specs=vmem,
         scratch_shapes=[
             pltpu.VMEM((2,) + gate_matrix.shape, bf16),
             pltpu.VMEM((2,) + up_matrix.shape, bf16),
             pltpu.VMEM((2,) + down_matrix.shape, bf16),
             pltpu.VMEM(gain.shape, f32),
-            pltpu.VMEM(dense.shape[1:], f32),
-            pltpu.VMEM((depth + 3,) + dense.shape[1:], f32),
-            pltpu.VMEM((depth + 3,) + dense.shape[1:], f32),
+            pltpu.VMEM(table, f32),
+            pltpu.VMEM((depth + 3,) + table, f32),
+            pltpu.VMEM((depth + 3,) + table, f32),
             pltpu.VMEM((2, depth, rows, main), bf16),
             pltpu.VMEM((2, depth, 4, cap, main), bf16),
             pltpu.VMEM((2, depth, 4, cap, main), bf16),
-            pltpu.VMEM((2, depth, 4, cap, main), bf16),
-            pltpu.VMEM((2, depth, 4, cap, main), bf16),
-            pltpu.VMEM((2, depth, rows, main), bf16),
-            pltpu.VMEM((2, 2, rows, main), bf16),
-            pltpu.VMEM((2, 2, rows, main), bf16),
-            pltpu.VMEM((2, 4, rows, rest), bf16),
-            pltpu.VMEM((2, 4, depth - 1, cap, rest), bf16),
-            pltpu.VMEM((2, depth, 4, cap, rest), bf16),
-            pltpu.VMEM((2, depth - 1, 4, cap, rest), bf16),
-            pltpu.VMEM((2, depth, 4, cap, rest), bf16),
-            pltpu.VMEM((2, 4, rows, rest), bf16),
-            pltpu.VMEM((2, 4, rows, rest), bf16),
-            pltpu.VMEM((2, rows, main), f32),
+            pltpu.VMEM((2, depth, 4, cap, back), bf16),
+            pltpu.VMEM((2, depth, 4, cap, back), bf16),
+            pltpu.VMEM((2, depth, rows, back), bf16),
+            pltpu.VMEM((2, 2, rows, back), bf16),
+            pltpu.VMEM((2, 2, rows, back), bf16),
+            pltpu.VMEM((2, 4, rows, width - main), bf16),
+            pltpu.VMEM((2, 4, depth - 1, cap, width - main), bf16),
+            pltpu.VMEM((2, depth, 4, cap, width - main), bf16),
+            pltpu.VMEM((2, depth - 1, 4, cap, width - back), bf16),
+            pltpu.VMEM((2, depth, 4, cap, width - back), bf16),
+            pltpu.VMEM((2, 4, rows, width - back), bf16),
+            pltpu.VMEM((2, 4, rows, width - back), bf16),
+            pltpu.VMEM((2, rows, back), f32),
             pltpu.VMEM((rows, width), f32),
-            pltpu.VMEM((2, rows, width), bf16),
+            pltpu.VMEM((2,) + table, f32),
             sems((9,)),
             sems((6,)),
             sems((depth + 3,)),
@@ -612,7 +635,7 @@
             has_side_effects=True,
             vmem_limit_bytes=60 * 1024 * 1024,
         ),
-    )(tokens, gain, dense, gate_matrix, up_matrix, down_matrix)
+    )(tokens, gain, place, ids, route, gate_matrix, up_matrix, down_matrix)
 
 
 def dense_local(
@@ -622,28 +645,19 @@
     section_index = lax.axis_index("section")
     tok_rows, top_count = expert_ids.shape[2:]
     cap = 5 * tok_rows * top_count // (4 * groups)
-    experts = jnp.arange(groups, dtype=jnp.int32)
-    held_by = jnp.sum(
-        jnp.where(expert_ids[0][..., None] == experts, expert_place[0], 0), axis=-1
-    )
-    holders = jnp.arange(2 * groups, dtype=jnp.int32) - groups * section_index
-    dense = jnp.sum(
-        jnp.where(
-            held_by[:, None] == holders[:, None, None], route_weights[0][:, None], 0.0
-        ),
-        axis=-1,
-    )
-    dense = jnp.pad(dense, ((0, 0), (0, 0), (0, -tok_rows % 128)))
-    return cascade_call(
+    finals = cascade_call(
         tokens,
         norm_gain,
-        dense,
+        expert_place,
+        jnp.swapaxes(expert_ids[0], 1, 2),
+        jnp.swapaxes(route_weights[0], 1, 2),
         gate_weight[0, 0],
         up_weight[0, 0],
         down_weight[0, 0],
         groups // 4,
         cap,
     )
+    return jnp.where(section_index == 0, finals, finals[::-1])
 
 
 def local(

time: 129 us -> 126 us (0.977)
  local copies, waits for them, and re-layouts: 2.5 us -> 0 us
  Pallas kernels: 125 us -> 123 us
    select_n x0 -> x1, other arithmetic: none -> 2.13 us  [dense_local(): return jnp.where(section_index == 0, finals, finals[::-1])]
    unnamed x1 -> x0, local copies, waits for them, and re-layouts: 1.88 us -> none
    reduce_sum x2 -> x0, other arithmetic: 1.67 us -> none  [the longest x1 0.85 us: dense_local(): jnp.sum(jnp.where(held_by[:, None] == holders[:, None, None], route_weigh...]
where the time goes in v4:
time: 126 us; the launch traced here: 125 us
  Pallas kernels  123 us (98%)
  other arithmetic  2.13 us (2%)
    pallas_call x1, Pallas kernels, cascade_call(): pl.pallas_call(functools.partial(cascade_kernel, depth, cap), out_shape=j...  123 us

profile of v4, /device:TPU:0, one launch (start us, length us, event | category | flops | bytes accessed | tf_op | source)
XLA Modules:
  0.0 125.5 jit_solution(3974520840455374653)
XLA Ops:
  0.0 123.3 %shard_map.82 = bf16[2,64,2048]{2,1,0:T(8,128)(2,1)} custom-call(bf16[2,64,2048]{2,1,0:T(8,128)(2,1)} %tokens_ref.1, f32[1,2048]{1,0:T(1,128)} %gain_ref.1, s32[1,16]{1,0:T(1,128)} %place_ref.1, s32[2,8,64]{2,1,0:T(8,128)} %bitcast.12, f32[2,8,64]{2,1,0:T(8,128)} %bitcast.13, bf16[2048,768]{1,0:T(8,128)(2,1)} %bitcast.9, bf16[2048,768]{1,0:T(8,128)(2,1)} %bitcast.10, ...), custom_call_target="tpu_custom_call" | custom-call | tf_op jit(solution)/shard_map/pallas_call | solution.py:580
  123.4 2.1 %reverse_select_fusion = bf16[2,64,2048]{2,1,0:T(8,128)(2,1)} fusion(bf16[2,64,2048]{2,1,0:T(8,128)(2,1)} %shard_map.82, pred[]{:T(512)S(6)} %eq.3), kind=kLoop, calls=%fused_computation | loop fusion | flops 262144 | bytes 1048577 | tf_op jit(solution)/shard_map/jit(_where)/select_n | solution.py:660
